TPU v7x, 32 devices: a whole 2x2x4 slice. The times are simulated.
32 devices in a mesh: tm: 16 (over z, y, x), space: 2 (over core).
Axes of the slice: x: 2, y: 2, z: 4, core: 2. Of those that a mesh axis runs over, the one named last changes fastest.
Arguments:
- links: float32 [2, 3, 3, 64, 8192], P(None, None, None, 'tm', 'space'), may hold values from -1 to 1, as said below
Outputs:
- ploop: float32 [2, 8192], P(None, ('space', 'tm'))
- loop_stats: float32 [3], replicated
Inputs may be any that keep to these rules, and one draw needn't show every extreme that they name: `links`: every link matrix is special unitary.
All inputs are finite; a program needn't handle non-finite values.
Results may differ from a plain program's by a relative error of at most 0.00014.
Values sent between devices are 32-bit elements; how exact they have to be, the bound alone decides.
A program may use at most 64 MiB of HBM per device.

v0:
```python
import jax
import jax.numpy as jnp
from jax import lax
from jax.sharding import PartitionSpec as P


def partner(block, axis, stride):
    count = lax.axis_size(axis)
    route = []
    for low in range(count):
        high = low | 1 << stride
        if high != low and high < count:
            route += [(low, high), (high, low)]
    return lax.ppermute(block, axis, route)


def cmul(left, right):

    def prod(first, second):
        return jnp.sum(first[:, :, None, :] * second[None, :, :, :], axis=1)

    return jnp.stack(
        [
            prod(left[0], right[0]) - prod(left[1], right[1]),
            prod(left[0], right[1]) + prod(left[1], right[0]),
        ]
    )


def trace_third(whole):
    return (whole[:, 0, 0] + whole[:, 1, 1] + whole[:, 2, 2]) / 3.0


def on_device(links):

    def step(index, acc):
        return cmul(acc, lax.dynamic_index_in_dim(links, index, 3, keepdims=False))

    local = lax.fori_loop(1, links.shape[3], step, links[:, :, :, 0, :])
    sites = links.shape[4]
    slabs = lax.axis_size("tm")
    share = sites // slabs
    position = lax.axis_index("tm")
    mine = local
    for level in range(slabs.bit_length() - 1):
        other = partner(mine, "tm", level)
        lower = position >> level & 1 == 0
        mine = cmul(jnp.where(lower, mine, other), jnp.where(lower, other, mine))
    ploop = trace_third(mine)
    mine_out = lax.dynamic_slice_in_dim(ploop, position * share, share, 1)
    total_sites = sites * lax.axis_size("space")
    sum_re, sum_im, sum_sq = lax.psum(
        (jnp.sum(ploop[0]), jnp.sum(ploop[1]), jnp.sum(ploop[0] * ploop[0] + ploop[1] * ploop[1])),
        "space",
    )
    mean_re = sum_re / total_sites
    mean_im = sum_im / total_sites
    square = sum_sq / total_sites
    stats = jnp.stack([mean_re, mean_im, square - mean_re * mean_re - mean_im * mean_im])
    return (mine_out, stats)


def solution(mesh):
    return jax.shard_map(
        on_device,
        mesh=mesh,
        in_specs=(P(None, None, None, "tm", "space"),),
        out_specs=(P(None, ("space", "tm")), P()),
        check_vma=False,
    )
```

profile of v0, /device:TPU:0, one launch (start us, length us, event | category | flops | bytes accessed | tf_op | source)
XLA Modules:
  0.0 74.7 jit_solution(1708581865336003553)
XLA Ops:
  0.6 1.5 %slice.134 = f32[2,3,3,1,4096]{4,3,2,1,0:T(1,128)S(1)} slice(f32[2,3,3,4,4096]{4,3,2,1,0:T(4,128)} %param.3), slice={[0:2], [0:3], [0:3], [0:1], [0:4096]} | slice | bytes 589824 | tf_op jit(solution)/shard_map/slice | solution.py:39
  2.3 8.2 %while.15 = (s32[]{:T(128)}, f32[2,3,3,4096]{3,2,1,0:T(4,128)S(1)}, f32[2,3,3,4,4096]{4,3,2,1,0:T(4,128)}, s32[]{:T(128)}, s32[]{:T(128)}, /*index=5*/s32[]{:T(128)}, s32[]{}) while((s32[]{:T(128)}, f32[2,3,3,4096]{3,2,1,0:T(4,128)S(1)}, f32[2,3,3,4,4096]{4,3,2,1,0:T(4,128)}, s32[]{:T(128)}, s32[]{:T(128)}, /*index=5*/s32[]{:T(128)}, s32[]{}) %tuple.86), condition=%wide.region_5.6_spmd, body=%wide.region_0.5_spmd.sunk | while | flops 884742 | bytes 4423819 | solution.py:39
  2.3 1.6 %constant_dynamic-slice_fusion.4 = (f32[1,3,3,1,4096]{4,3,2,1,0:T(1,128)S(1)}, f32[1,3,3,1,4096]{4,3,2,1,0:T(1,128)S(1)}) fusion(f32[2,3,3,4,4096]{4,3,2,1,0:T(4,128)} %get-tuple-element.213, s32[]{:T(128)S(6)} %select_n.86, s32[]{:T(128)S(6)} %add.162), kind=kLoop, calls=%fused_computation.11.clone.1 | loop fusion | bytes 589832 | tf_op jit(solution)/shard_map/while/body/eval_jaxpr/slice | solution.py:24
  4.2 0.6 multiply_reduce_fusion.21
  5.1 1.6 %constant_dynamic-slice_fusion.4 = (f32[1,3,3,1,4096]{4,3,2,1,0:T(1,128)S(1)}, f32[1,3,3,1,4096]{4,3,2,1,0:T(1,128)S(1)}) fusion(f32[2,3,3,4,4096]{4,3,2,1,0:T(4,128)} %get-tuple-element.213, s32[]{:T(128)S(6)} %select_n.86, s32[]{:T(128)S(6)} %add.162), kind=kLoop, calls=%fused_computation.11.clone.1 | loop fusion | bytes 589832 | tf_op jit(solution)/shard_map/while/body/eval_jaxpr/slice | solution.py:24
  6.9 0.6 multiply_reduce_fusion.21
  7.8 1.6 %constant_dynamic-slice_fusion.4 = (f32[1,3,3,1,4096]{4,3,2,1,0:T(1,128)S(1)}, f32[1,3,3,1,4096]{4,3,2,1,0:T(1,128)S(1)}) fusion(f32[2,3,3,4,4096]{4,3,2,1,0:T(4,128)} %get-tuple-element.213, s32[]{:T(128)S(6)} %select_n.86, s32[]{:T(128)S(6)} %add.162), kind=kLoop, calls=%fused_computation.11.clone.1 | loop fusion | bytes 589832 | tf_op jit(solution)/shard_map/while/body/eval_jaxpr/slice | solution.py:24
  9.7 0.6 multiply_reduce_fusion.21
  10.6 3.0 %collective-permute-start = (f32[2,3,3,4096]{3,2,1,0:T(4,128)S(1)}, f32[2,3,3,4096]{3,2,1,0:T(4,128)S(1)}, u32[]{:S(2)}, u32[]{:S(2)}) collective-permute-start(f32[2,3,3,4096]{3,2,1,0:T(4,128)S(1)} %get-tuple-element.90), channel_id=1, source_target_pairs={{0,2},{2,0},{4,6},{6,4},{8,10},{10,8},{12,14},{14,12},{16,18},{18,... | collective-permute-start | bytes 884744 | tf_op jit(solution)/shard_map/ppermute | solution.py:14
  13.6 9.1 %collective-permute-done = f32[2,3,3,4096]{3,2,1,0:T(4,128)S(1)} collective-permute-done((f32[2,3,3,4096]{3,2,1,0:T(4,128)S(1)}, f32[2,3,3,4096]{3,2,1,0:T(4,128)S(1)}, u32[]{:S(2)}, u32[]{:S(2)}) %collective-permute-start) | collective-permute-done | bytes 294944 | tf_op jit(solution)/shard_map/ppermute | solution.py:14
  23.0 0.6 multiply_reduce_fusion.18
  23.9 1.8 %collective-permute-start.1 = (f32[2,3,3,4096]{3,2,1,0:T(4,128)S(1)}, f32[2,3,3,4096]{3,2,1,0:T(4,128)S(1)}, u32[]{:S(2)}, u32[]{:S(2)}) collective-permute-start(f32[2,3,3,4096]{3,2,1,0:T(4,128)S(1)} %pad_maximum_fusion.1), channel_id=1, source_target_pairs={{0,4},{4,0},{2,6},{6,2},{8,12},{12,8},{10,14},{14,10},{16,20},{20,... | collective-permute-start | bytes 884744 | tf_op jit(solution)/shard_map/ppermute | solution.py:14
  25.7 8.5 %collective-permute-done.1 = f32[2,3,3,4096]{3,2,1,0:T(4,128)S(1)} collective-permute-done((f32[2,3,3,4096]{3,2,1,0:T(4,128)S(1)}, f32[2,3,3,4096]{3,2,1,0:T(4,128)S(1)}, u32[]{:S(2)}, u32[]{:S(2)}) %collective-permute-start.1) | collective-permute-done | bytes 294944 | tf_op jit(solution)/shard_map/ppermute | solution.py:14
  34.6 0.6 multiply_reduce_fusion.14
  35.4 1.6 %collective-permute-start.2 = (f32[2,3,3,4096]{3,2,1,0:T(4,128)S(1)}, f32[2,3,3,4096]{3,2,1,0:T(4,128)S(1)}, u32[]{:S(2)}, u32[]{:S(2)}) collective-permute-start(f32[2,3,3,4096]{3,2,1,0:T(4,128)S(1)} %pad_maximum_fusion.2), channel_id=1, source_target_pairs={{0,8},{8,0},{2,10},{10,2},{4,12},{12,4},{6,14},{14,6},{16,24},{24,... | collective-permute-start | bytes 884744 | tf_op jit(solution)/shard_map/ppermute | solution.py:14
  37.0 7.9 %collective-permute-done.2 = f32[2,3,3,4096]{3,2,1,0:T(4,128)S(1)} collective-permute-done((f32[2,3,3,4096]{3,2,1,0:T(4,128)S(1)}, f32[2,3,3,4096]{3,2,1,0:T(4,128)S(1)}, u32[]{:S(2)}, u32[]{:S(2)}) %collective-permute-start.2) | collective-permute-done | bytes 294944 | tf_op jit(solution)/shard_map/ppermute | solution.py:14
  45.3 0.6 multiply_reduce_fusion.10
  46.1 2.3 %collective-permute-start.3 = (f32[2,3,3,4096]{3,2,1,0:T(4,128)S(1)}, f32[2,3,3,4096]{3,2,1,0:T(4,128)S(1)}, u32[]{:S(2)}, u32[]{:S(2)}) collective-permute-start(f32[2,3,3,4096]{3,2,1,0:T(4,128)S(1)} %pad_maximum_fusion.3), channel_id=1, source_target_pairs={{0,16},{16,0},{2,18},{18,2},{4,20},{20,4},{6,22},{22,6},{8,24},{24... | collective-permute-start | bytes 884744 | tf_op jit(solution)/shard_map/ppermute | solution.py:14
  48.5 15.6 %collective-permute-done.3 = f32[2,3,3,4096]{3,2,1,0:T(4,128)S(1)} collective-permute-done((f32[2,3,3,4096]{3,2,1,0:T(4,128)S(1)}, f32[2,3,3,4096]{3,2,1,0:T(4,128)S(1)}, u32[]{:S(2)}, u32[]{:S(2)}) %collective-permute-start.3) | collective-permute-done | bytes 294944 | tf_op jit(solution)/shard_map/ppermute | solution.py:14
  64.4 0.6 multiply_reduce_fusion.6
  65.3 0.7 slice_reduce_fusion
  66.0 3.2 %all-reduce = (f32[]{:T(128)}, f32[]{:T(128)}, f32[]{:T(128)}) all-reduce(f32[]{:T(128)} %get-tuple-element.115, f32[]{:T(128)} %get-tuple-element.116, f32[]{:T(128)} %get-tuple-element.114), channel_id=1, replica_groups=mesh['tm'=16,'space'=2] {'space'}, use_global_device_ids=true, to_apply=%region_27.28 | all-reduce | flops 3 | bytes 24 | tf_op jit(solution)/shard_map/psum | solution.py:52
  72.8 0.6 copy.16
  74.1 0.6 pad_maximum_fusion.5
  (40 shorter events, 3.7 us)
Async XLA Ops:
  10.6 12.1 %collective-permute-start = (f32[2,3,3,4096]{3,2,1,0:T(4,128)S(1)}, f32[2,3,3,4096]{3,2,1,0:T(4,128)S(1)}, u32[]{:S(2)}, u32[]{:S(2)}) collective-permute-start(f32[2,3,3,4096]{3,2,1,0:T(4,128)S(1)} %get-tuple-element.90), channel_id=1, source_target_pairs={{0,2},{2,0},{4,6},{6,4},{8,10},{10,8},{12,14},{14,12},{16,18},{18,... | collective-permute-start | bytes 884744 | tf_op jit(solution)/shard_map/ppermute | solution.py:14
  23.9 10.3 %collective-permute-start.1 = (f32[2,3,3,4096]{3,2,1,0:T(4,128)S(1)}, f32[2,3,3,4096]{3,2,1,0:T(4,128)S(1)}, u32[]{:S(2)}, u32[]{:S(2)}) collective-permute-start(f32[2,3,3,4096]{3,2,1,0:T(4,128)S(1)} %pad_maximum_fusion.1), channel_id=1, source_target_pairs={{0,4},{4,0},{2,6},{6,2},{8,12},{12,8},{10,14},{14,10},{16,20},{20,... | collective-permute-start | bytes 884744 | tf_op jit(solution)/shard_map/ppermute | solution.py:14
  35.4 9.5 %collective-permute-start.2 = (f32[2,3,3,4096]{3,2,1,0:T(4,128)S(1)}, f32[2,3,3,4096]{3,2,1,0:T(4,128)S(1)}, u32[]{:S(2)}, u32[]{:S(2)}) collective-permute-start(f32[2,3,3,4096]{3,2,1,0:T(4,128)S(1)} %pad_maximum_fusion.2), channel_id=1, source_target_pairs={{0,8},{8,0},{2,10},{10,2},{4,12},{12,4},{6,14},{14,6},{16,24},{24,... | collective-permute-start | bytes 884744 | tf_op jit(solution)/shard_map/ppermute | solution.py:14
  46.1 18.0 %collective-permute-start.3 = (f32[2,3,3,4096]{3,2,1,0:T(4,128)S(1)}, f32[2,3,3,4096]{3,2,1,0:T(4,128)S(1)}, u32[]{:S(2)}, u32[]{:S(2)}) collective-permute-start(f32[2,3,3,4096]{3,2,1,0:T(4,128)S(1)} %pad_maximum_fusion.3), channel_id=1, source_target_pairs={{0,16},{16,0},{2,18},{18,2},{4,20},{20,4},{6,22},{22,6},{8,24},{24... | collective-permute-start | bytes 884744 | tf_op jit(solution)/shard_map/ppermute | solution.py:14
where the time goes:
time: 75 us; the launch traced here: 74.7 us
  waiting for transfers between devices  41.1 us (55%)
  starting transfers between devices  8.82 us (12%)
  local copies, waits for them, and re-layouts  8.34 us (11%)
  other arithmetic  7.81 us (10%)
  between operations  5.2 us (7%)
  blocking collectives  3.16 us (4%)
    ppermute x4, waiting for transfers between devices, partner(): return lax.ppermute(block, axis, route)  41.1 us
    ppermute x4, starting transfers between devices, partner(): return lax.ppermute(block, axis, route)  8.82 us
    slice x3, local copies, waits for them, and re-layouts, cmul(): right[0]  4.66 us
    reduce_sum x7, other arithmetic, prod(): return jnp.sum(first[:, :, None, :] * second[None, :, :, :], axis=1)  4.43 us
    psum x1, blocking collectives, on_device(): lax.psum((jnp.sum(ploop[0]), jnp.sum(ploop[1]), jnp.sum(ploop[0] * ploop[...  3.16 us
  transfers between devices with their start and end apart: 4, of which 4 were waited for; matrix products, arithmetic and copies ran while one was open for 0% of the time, Pallas kernels for 0%

commit v1 on v0

v1 whole, which is shorter than its diff:
```python
import functools
import math

import jax
import jax.numpy as jnp
from jax import lax
from jax.experimental import pallas as pl
from jax.experimental.pallas import tpu as pltpu
from jax.sharding import PartitionSpec as P

MESH = pl.DeviceIdType.MESH
LANES = 128


def xor(index, flip):
    out, bit = 0, 1
    while bit <= flip:
        digit = index // bit % 2
        out = out + (bit * (1 - digit) if flip & bit else bit * digit)
        bit *= 2
    return out + index // bit * bit


def cmul(a, b):
    return (a[0] * b[0] - a[1] * b[1], a[0] * b[1] + a[1] * b[0])


def times(left, right):
    out = []
    for row in left:
        new = []
        for k in range(3):
            terms = [cmul(row[j], right[j][k]) for j in range(3)]
            new.append((terms[0][0] + terms[1][0] + terms[2][0], terms[0][1] + terms[1][1] + terms[2][1]))
        out.append(new)
    return out


def whole(rows):
    first, second = rows
    third = []
    for k in range(3):
        i, j = (k + 1) % 3, (k + 2) % 3
        p, q = cmul(first[i], second[j]), cmul(first[j], second[i])
        third.append((p[0] - q[0], q[1] - p[1]))
    return [first, second, third]


def take(block, rows):
    return [[(block[i * 3 + j], block[(rows + i) * 3 + j]) for j in range(3)] for i in range(rows)]


def flat(rows):
    return [x[part] for part in range(2) for row in rows for x in row]


def product(parts):
    while len(parts) > 1:
        merged = [times(parts[n], whole(parts[n + 1])) for n in range(0, len(parts) - 1, 2)]
        parts = merged + parts[2 * len(merged):]
    return parts[0]


def kernel(tm, space, low, high, nt, rows, share, total_sites,
           links, ploop, stats,
           staged, send1, recv1, send2, recv2, mine, others,
           in_sem, send_sem1, recv_sem1, send_sem2, recv_sem2, send_sem3, recv_sem3):
    me_tm, me_space = lax.axis_index("tm"), lax.axis_index("space")
    lo, hi = me_tm % low, me_tm // low
    me = me_tm * space + me_space
    count = tm * space
    band = high * rows

    def chunk_copies(slot, target):
        return [
            pltpu.make_async_copy(
                links.at[:, h, target], staged.at[slot, :, pl.ds(h * rows * nt, rows * nt), :], in_sem.at[slot]
            )
            for h in range(high)
        ]

    flips = [low - 1] + list(range(1, low - 1)) + [0] if low > 1 else [0]
    targets = [xor(lo, flip) for flip in flips]
    for slot, target in enumerate(targets):
        for copy in chunk_copies(slot, target):
            copy.start()

    barrier = pltpu.get_barrier_semaphore()

    def greet(step, carry):
        other = (me + step) % count
        pl.semaphore_signal(barrier, inc=1, device_id=(other // space, other % space), device_id_type=MESH)
        return carry

    lax.fori_loop(1, count, greet, 0, unroll=count <= 64)

    sends1 = []
    for slot, target in enumerate(targets):
        pltpu.make_async_copy(staged.at[slot], staged.at[slot], in_sem.at[slot]).wait()

        def matrix(t, count_rows):
            block = {}
            for part in range(2):
                for i in range(count_rows):
                    for j in range(3):
                        block[(part * count_rows + i) * 3 + j] = staged[
                            slot, part * 9 + i * 3 + j, pl.ds(t, band, stride=nt), :
                        ]
            return take(block, count_rows)

        acc = matrix(0, 2)
        for t in range(1, nt):
            acc = times(acc, matrix(t, 3))
        own = slot == len(targets) - 1
        for c, value in enumerate(flat(acc)):
            if own:
                recv1[lo, c] = value
            else:
                send1[slot, c] = value
        if slot == 0:
            pl.semaphore_wait(barrier, count - 1)
        if not own:
            copy = pltpu.make_async_remote_copy(
                src_ref=send1.at[slot], dst_ref=recv1.at[lo],
                send_sem=send_sem1.at[slot], recv_sem=recv_sem1.at[slot],
                device_id=(hi * low + target, me_space), device_id_type=MESH,
            )
            copy.start()
            sends1.append(copy)
    for copy in sends1:
        copy.wait_recv()

    acc = product([take([recv1[src, c] for c in range(12)], 2) for src in range(low)])
    for c, value in enumerate(flat(acc)):
        for h in range(high):
            send2[h, c] = value[h * rows:(h + 1) * rows, :]

    own2 = send2.at[hi]
    sends2 = []
    flips2 = list(range(high - 1, 0, -1))
    for slot, flip in enumerate(flips2):
        target = xor(hi, flip)
        copy = pltpu.make_async_remote_copy(
            src_ref=send2.at[target], dst_ref=recv2.at[hi],
            send_sem=send_sem2.at[slot], recv_sem=recv_sem2.at[slot],
            device_id=(target * low + lo, me_space), device_id_type=MESH,
        )
        copy.start()
        sends2.append(copy)
    for c in range(12):
        recv2[hi, c] = own2[c]
    for copy in sends2:
        copy.wait_recv()

    parts = [take([recv2[src, c] for c in range(12)], 2) for src in range(high)]
    half = max(high // 2, 1)
    left = whole(product(parts[:half]))
    if high > 1:
        right = whole(product(parts[half:]))
        terms = [cmul(left[i][j], right[j][i]) for i in range(3) for j in range(3)]
    else:
        terms = [left[i][i] for i in range(3)]
    re = functools.reduce(jnp.add, [x[0] for x in terms]) / 3.0
    im = functools.reduce(jnp.add, [x[1] for x in terms]) / 3.0
    mine[0:1, :] = jnp.sum(re, axis=0, keepdims=True)
    mine[1:2, :] = jnp.sum(im, axis=0, keepdims=True)
    mine[2:3, :] = jnp.sum(re * re + im * im, axis=0, keepdims=True)
    mine[3:4, :] = jnp.zeros((1, LANES), jnp.float32)

    def spread(step, carry):
        other = (me + step) % count
        pltpu.make_async_remote_copy(
            src_ref=mine, dst_ref=others.at[step - 1], send_sem=send_sem3, recv_sem=recv_sem3,
            device_id=(other // space, other % space), device_id_type=MESH,
        ).start()
        return carry

    lax.fori_loop(1, count, spread, 0, unroll=count <= 64)
    for r in range(rows):
        width = min(LANES, share - r * LANES)
        if width > 0:
            ploop[0:1, r * LANES:r * LANES + width] = re[r:r + 1, :width]
            ploop[1:2, r * LANES:r * LANES + width] = im[r:r + 1, :width]
    for copy in sends1 + sends2:
        copy.wait_send()
    pltpu.make_async_copy(others, others, recv_sem3).wait()
    sums = jnp.sum(others[...], axis=0) + mine[...]
    mean_re = jnp.sum(sums[0:1, :]) / total_sites
    mean_im = jnp.sum(sums[1:2, :]) / total_sites
    square = jnp.sum(sums[2:3, :]) / total_sites
    stats[0] = mean_re
    stats[1] = mean_im
    stats[2] = square - mean_re * mean_re - mean_im * mean_im
    pltpu.make_async_copy(others, others, send_sem3).wait()


def on_device(tm, space, links):
    nt, sites = links.shape[3], links.shape[4]
    share = sites // tm
    unit = LANES * (8 // math.gcd(8, nt))
    padded = -(-share // unit) * unit
    rows = padded // LANES
    low = 1 << (tm.bit_length() - 1) // 2
    high = tm // low
    view = links.reshape(18, nt, tm, share)
    if padded != share:
        view = jnp.pad(view, ((0, 0), (0, 0), (0, 0), (0, padded - share)))
    view = view.reshape(18, nt, tm * rows, LANES).transpose(0, 2, 1, 3)
    view = view.reshape(18, high, low, rows * nt, LANES)
    band = high * rows
    count = tm * space
    f32 = jnp.float32
    peers1, peers2 = max(low - 1, 1), max(high - 1, 1)
    return pl.pallas_call(
        functools.partial(kernel, tm, space, low, high, nt, rows, share, sites * space),
        out_shape=(jax.ShapeDtypeStruct((2, share), f32), jax.ShapeDtypeStruct((3,), f32)),
        in_specs=[pl.BlockSpec(memory_space=pl.ANY)],
        out_specs=(pl.BlockSpec(memory_space=pltpu.VMEM), pl.BlockSpec(memory_space=pltpu.SMEM)),
        scratch_shapes=[
            pltpu.VMEM((low, 18, band * nt, LANES), f32),
            pltpu.VMEM((peers1, 12, band, LANES), f32),
            pltpu.VMEM((low, 12, band, LANES), f32),
            pltpu.VMEM((high, 12, rows, LANES), f32),
            pltpu.VMEM((high, 12, rows, LANES), f32),
            pltpu.VMEM((4, LANES), f32),
            pltpu.VMEM((count - 1, 4, LANES), f32),
            pltpu.SemaphoreType.DMA((low,)),
            pltpu.SemaphoreType.DMA((peers1,)),
            pltpu.SemaphoreType.DMA((peers1,)),
            pltpu.SemaphoreType.DMA((peers2,)),
            pltpu.SemaphoreType.DMA((peers2,)),
            pltpu.SemaphoreType.DMA,
            pltpu.SemaphoreType.DMA,
        ],
        compiler_params=pltpu.CompilerParams(collective_id=0, has_side_effects=True),
    )(view)


def solution(mesh):
    return jax.shard_map(
        functools.partial(on_device, mesh.shape["tm"], mesh.shape["space"]),
        mesh=mesh,
        in_specs=(P(None, None, None, "tm", "space"),),
        out_specs=(P(None, ("space", "tm")), P()),
        check_vma=False,
    )
```

time: 75 us -> 23.3 us (0.31)
  waiting for transfers between devices: 41.1 us -> 0 us
  Pallas kernels: 0 us -> 20.1 us
  starting transfers between devices: 8.82 us -> 0 us
  other arithmetic: 7.81 us -> 0 us
  local copies, waits for them, and re-layouts: 8.34 us -> 2.39 us
  between operations: 5.2 us -> 0.64 us
  blocking collectives: 3.16 us -> 0 us
    ppermute x4 -> x0, waiting for transfers between devices: 41.1 us -> none  [partner(): return lax.ppermute(block, axis, route)]
    pallas_call x0 -> x1, Pallas kernels: none -> 20.1 us  [on_device(): pl.pallas_call(functools.partial(kernel, tm, space, low, high, nt, rows,...]
    ppermute x4 -> x0, starting transfers between devices: 8.82 us -> none  [partner(): return lax.ppermute(block, axis, route)]
    slice x4 -> x0, local copies, waits for them, and re-layouts: 6.14 us -> none  [the longest x3 4.66 us: cmul(): right[0]]
    reduce_sum x8 -> x0, other arithmetic: 5.11 us -> none  [the longest x7 4.43 us: prod(): return jnp.sum(first[:, :, None, :] * second[None, :, :, :], axis=1)]
    psum x1 -> x0, blocking collectives: 3.16 us -> none  [on_device(): lax.psum((jnp.sum(ploop[0]), jnp.sum(ploop[1]), jnp.sum(ploop[0] * ploop[...]
    unnamed x2, local copies, waits for them, and re-layouts: 0.79 us -> 2.39 us
    mul x13 -> x0, local copies, waits for them, and re-layouts: 1.4 us -> none  [prod(): return jnp.sum(first[:, :, None, :] * second[None, :, :, :], axis=1)]
  transfers between devices with their start and end apart: 4 -> 0, of which waited for: 4 -> 0; matrix products, arithmetic and copies ran while one was open for 0% -> 0% of each run, Pallas kernels for 0% -> 0%
where the time goes in v1:
time: 23.3 us; the launch traced here: 23.1 us
  Pallas kernels  20.1 us (86%)
  local copies, waits for them, and re-layouts  2.39 us (10%)
  between operations  0.64 us (3%)
    pallas_call x1, Pallas kernels, on_device(): pl.pallas_call(functools.partial(kernel, tm, space, low, high, nt, rows,...  20.1 us
    unnamed x2, local copies, waits for them, and re-layouts  2.39 us

profile of v1, /device:TPU:0, one launch (start us, length us, event | category | flops | bytes accessed | tf_op | source)
XLA Modules:
  0.0 23.1 jit_solution(2370320602788256494)
XLA Ops:
  0.6 20.1 %shard_map.30 = (f32[2,256]{1,0:T(2,128)}, f32[3]{0:T(128)}) custom-call(f32[18,4,4,8,128]{4,3,2,1,0:T(8,128)} %bitcast.5), custom_call_target="tpu_custom_call" | custom-call | tf_op jit(solution)/shard_map/pallas_call | solution.py:214
  20.7 1.2 %copy.6 = f32[2,256]{1,0:T(2,128)} copy(f32[2,256]{1,0:T(2,128)} %get-tuple-element.4) | data formatting | bytes 4096
  22.0 1.1 %copy.7 = f32[3]{0:T(128)} copy(f32[3]{0:T(128)} %get-tuple-element.5) | data formatting | bytes 24

commit v2 on v1

v2 whole, which is shorter than its diff:
```python
import functools
import math

import jax
import jax.numpy as jnp
from jax import lax
from jax.experimental import pallas as pl
from jax.experimental.pallas import tpu as pltpu
from jax.sharding import PartitionSpec as P

MESH = pl.DeviceIdType.MESH
LANES = 128


def xor(index, flip):
    out, bit = 0, 1
    while bit <= flip:
        digit = index // bit % 2
        out = out + (bit * (1 - digit) if flip & bit else bit * digit)
        bit *= 2
    return out + index // bit * bit


def cmul(a, b):
    return (a[0] * b[0] - a[1] * b[1], a[0] * b[1] + a[1] * b[0])


def times(left, right):
    out = []
    for row in left:
        new = []
        for k in range(3):
            terms = [cmul(row[j], right[j][k]) for j in range(3)]
            new.append((terms[0][0] + terms[1][0] + terms[2][0], terms[0][1] + terms[1][1] + terms[2][1]))
        out.append(new)
    return out


def whole(rows):
    first, second = rows
    third = []
    for k in range(3):
        i, j = (k + 1) % 3, (k + 2) % 3
        p, q = cmul(first[i], second[j]), cmul(first[j], second[i])
        third.append((p[0] - q[0], q[1] - p[1]))
    return [first, second, third]


def take(block, rows):
    return [[(block[i * 3 + j], block[(rows + i) * 3 + j]) for j in range(3)] for i in range(rows)]


def flat(rows):
    return [x[part] for part in range(2) for row in rows for x in row]


def product(parts):
    while len(parts) > 1:
        merged = [times(parts[n], whole(parts[n + 1])) for n in range(0, len(parts) - 1, 2)]
        parts = merged + parts[2 * len(merged):]
    return parts[0]


def kernel(tm, space, low, high, nt, rows, share, total_sites,
           links, ploop, stats,
           staged, send1, recv1, send2, recv2, outbox, inbox, mine, others, shadow,
           in_sem, send_sem1, recv_sem1, send_sem2, recv_sem2, send_sem3, recv_sem3, send_sem4, recv_sem4):
    me_tm, me_space = lax.axis_index("tm"), lax.axis_index("space")
    lo, hi = me_tm % low, me_tm // low
    me = me_tm * space + me_space
    count = tm * space
    band = high * rows
    half = high // 2
    part = half * rows
    near = hi // half
    far = 1 - near
    order = (far, near)
    middles = (half - 1, half)
    voices = 2 * low * space

    def chunk_copies(slot, target):
        return [
            pltpu.make_async_copy(
                links.at[:, h, target], staged.at[slot, :, pl.ds(h * rows * nt, rows * nt), :], in_sem.at[slot]
            )
            for h in range(high)
        ]

    barrier = pltpu.get_barrier_semaphore()

    def greet(other_tm, other_space):
        pl.semaphore_signal(barrier, inc=1, device_id=(other_tm, other_space), device_id_type=MESH)

    for step in range(1, low):
        greet(hi * low + (lo + step) % low, me_space)
    for step in range(1, space):
        greet(me_tm, (me_space + step) % space)
    middle = (hi >= middles[0]) & (hi <= middles[1])

    @pl.when(middle)
    def _():
        for step in range(1, high):
            greet((hi + step) % high * low + lo, me_space)

    @pl.when(jnp.logical_not(middle))
    def _():
        for h in middles:
            greet(h * low + lo, me_space)

    flips = [low - 1] + list(range(1, low - 1)) + [0] if low > 1 else [0]
    targets = [xor(lo, flip) for flip in flips]
    for slot, target in enumerate(targets):
        for copy in chunk_copies(slot, target):
            copy.start()

    def send_half(slot, turn):
        copy = pltpu.make_async_remote_copy(
            src_ref=send1.at[slot, order[turn]], dst_ref=recv1.at[lo, order[turn]],
            send_sem=send_sem1.at[slot, turn], recv_sem=recv_sem1.at[slot, turn],
            device_id=(hi * low + targets[slot], me_space), device_id_type=MESH,
        )
        copy.start()
        return copy

    sends1 = ([], [])
    for slot, target in enumerate(targets):
        pltpu.make_async_copy(staged.at[slot], staged.at[slot], in_sem.at[slot]).wait()

        def matrix(t, count_rows):
            block = {}
            for p in range(2):
                for i in range(count_rows):
                    for j in range(3):
                        block[(p * count_rows + i) * 3 + j] = staged[
                            slot, p * 9 + i * 3 + j, pl.ds(t, band, stride=nt), :
                        ]
            return take(block, count_rows)

        acc = matrix(0, 2)
        for t in range(1, nt):
            acc = times(acc, matrix(t, 3))
        own = slot == len(targets) - 1
        for c, value in enumerate(flat(acc)):
            for k in range(2):
                if own:
                    recv1[lo, k, c] = value[k * part:(k + 1) * part, :]
                else:
                    send1[slot, k, c] = value[k * part:(k + 1) * part, :]
        if slot == 0:
            @pl.when(middle)
            def _():
                pl.semaphore_wait(barrier, low - 1 + space - 1 + high - 1)

            @pl.when(jnp.logical_not(middle))
            def _():
                pl.semaphore_wait(barrier, low - 1 + space - 1 + 2)
        if not own:
            sends1[0].append(send_half(slot, 0))
        if slot == len(targets) - 2:
            sends1[1].extend(send_half(k, 1) for k in range(len(targets) - 1))

    def send_product(turn):
        return pltpu.make_async_remote_copy(
            src_ref=send2.at[turn], dst_ref=recv2.at[hi],
            send_sem=send_sem2.at[turn], recv_sem=recv_sem2.at[hi],
            device_id=((half - 1 + order[turn]) * low + lo, me_space), device_id_type=MESH,
        )

    for turn in range(2):
        for copy in sends1[turn]:
            copy.wait_recv()
        acc = product([take([recv1[src, order[turn], c] for c in range(12)], 2) for src in range(low)])
        for c, value in enumerate(flat(acc)):
            send2[turn, c] = value
        if turn == 0:
            send_product(0).start()

    @pl.when(jnp.logical_not(middle))
    def _():
        send_product(1).start()

    def place(re, im):
        for r in range(rows):
            width = min(LANES, share - r * LANES)
            if width > 0:
                ploop[0:1, r * LANES:r * LANES + width] = re[r:r + 1, :width]
                ploop[1:2, r * LANES:r * LANES + width] = im[r:r + 1, :width]

    lane = lax.broadcasted_iota(jnp.int32, (1, LANES), 1)

    def finish():
        sums = jnp.sum(others[...], axis=0) / total_sites
        spread = jnp.where(lane < 2, -sums * sums, jnp.where(lane == 2, sums, 0.0))
        total = jnp.sum(spread, axis=1, keepdims=True)
        stats[...] = jnp.where(lane == 2, total, sums)[:, :3]

    for g in range(2):
        @pl.when(hi == middles[g])
        def _(g=g):
            parts = []
            for src in range(high):
                if src == middles[g]:
                    parts.append(take([send2[1, c] for c in range(12)], 2))
                    continue
                pltpu.make_async_copy(recv2.at[src], recv2.at[src], recv_sem2.at[src]).wait()
                parts.append(take([recv2[src, c] for c in range(12)], 2))
            left, right = whole(product(parts[:half])), whole(product(parts[half:]))
            terms = [cmul(left[i][j], right[j][i]) for i in range(3) for j in range(3)]
            re = functools.reduce(jnp.add, [x[0] for x in terms]) / 3.0
            im = functools.reduce(jnp.add, [x[1] for x in terms]) / 3.0
            row = jnp.zeros((1, LANES), jnp.float32)
            for k, value in enumerate((re, im, re * re + im * im)):
                value = jnp.sum(jnp.sum(value, axis=0, keepdims=True), axis=1, keepdims=True)
                row = jnp.where(lane == k, value, row)
            slot = (g * low + lo) * space + me_space
            mine[...] = row
            others[slot] = row

            def spread(step, carry):
                other = (me + step) % count
                pltpu.make_async_remote_copy(
                    src_ref=mine, dst_ref=others.at[slot], send_sem=send_sem3, recv_sem=recv_sem3,
                    device_id=(other // space, other % space), device_id_type=MESH,
                ).start()
                return carry

            lax.fori_loop(1, count, spread, 0, unroll=count <= 64)
            copies = []
            for k in range(half):
                owner = g * half + k
                real, imag = re[k * rows:(k + 1) * rows, :], im[k * rows:(k + 1) * rows, :]
                if owner == middles[g]:
                    place(real, imag)
                    continue
                outbox[k, 0] = real
                outbox[k, 1] = imag
                copy = pltpu.make_async_remote_copy(
                    src_ref=outbox.at[k], dst_ref=inbox, send_sem=send_sem4.at[k], recv_sem=recv_sem4,
                    device_id=(owner * low + lo, me_space), device_id_type=MESH,
                )
                copy.start()
                copies.append(copy)
            pltpu.make_async_copy(others.at[0:voices - 1], others.at[0:voices - 1], recv_sem3).wait()
            finish()
            for copy in copies:
                copy.wait_send()
            pltpu.make_async_copy(shadow, shadow, send_sem3).wait()

    @pl.when(jnp.logical_not(middle))
    def _():
        pltpu.make_async_copy(inbox, inbox, recv_sem4).wait()
        place(inbox[0], inbox[1])
        send_product(1).wait_send()
        pltpu.make_async_copy(others, others, recv_sem3).wait()
        finish()

    send_product(0).wait_send()
    for copy in sends1[0] + sends1[1]:
        copy.wait_send()


def on_device(tm, space, links):
    nt, sites = links.shape[3], links.shape[4]
    share = sites // tm
    unit = LANES * (8 // math.gcd(8, nt))
    padded = -(-share // unit) * unit
    rows = padded // LANES
    low = 1 << (tm.bit_length() - 1) // 2
    high = tm // low
    view = links.reshape(18, nt, tm, share)
    if padded != share:
        view = jnp.pad(view, ((0, 0), (0, 0), (0, 0), (0, padded - share)))
    view = view.reshape(18, nt, tm * rows, LANES).transpose(0, 2, 1, 3)
    view = view.reshape(18, high, low, rows * nt, LANES)
    band, part = high * rows, high // 2 * rows
    count = tm * space
    f32 = jnp.float32
    peers = max(low - 1, 1)
    ploop, stats = pl.pallas_call(
        functools.partial(kernel, tm, space, low, high, nt, rows, share, sites * space),
        out_shape=(jax.ShapeDtypeStruct((2, share), f32), jax.ShapeDtypeStruct((1, 3), f32)),
        in_specs=[pl.BlockSpec(memory_space=pl.ANY)],
        out_specs=(pl.BlockSpec(memory_space=pltpu.VMEM), pl.BlockSpec(memory_space=pltpu.VMEM)),
        scratch_shapes=[
            pltpu.VMEM((low, 18, band * nt, LANES), f32),
            pltpu.VMEM((peers, 2, 12, part, LANES), f32),
            pltpu.VMEM((low, 2, 12, part, LANES), f32),
            pltpu.VMEM((2, 12, part, LANES), f32),
            pltpu.VMEM((high, 12, part, LANES), f32),
            pltpu.VMEM((high // 2, 2, rows, LANES), f32),
            pltpu.VMEM((2, rows, LANES), f32),
            pltpu.VMEM((1, LANES), f32),
            pltpu.VMEM((2 * low * space, 1, LANES), f32),
            pltpu.VMEM((count - 1, 1, LANES), f32),
            pltpu.SemaphoreType.DMA((low,)),
            pltpu.SemaphoreType.DMA((peers, 2)),
            pltpu.SemaphoreType.DMA((peers, 2)),
            pltpu.SemaphoreType.DMA((2,)),
            pltpu.SemaphoreType.DMA((high,)),
            pltpu.SemaphoreType.DMA,
            pltpu.SemaphoreType.DMA,
            pltpu.SemaphoreType.DMA((high // 2,)),
            pltpu.SemaphoreType.DMA,
        ],
        compiler_params=pltpu.CompilerParams(collective_id=0, has_side_effects=True),
    )(view)
    return ploop, stats.reshape(3)


def solution(mesh):
    return jax.shard_map(
        functools.partial(on_device, mesh.shape["tm"], mesh.shape["space"]),
        mesh=mesh,
        in_specs=(P(None, None, None, "tm", "space"),),
        out_specs=(P(None, ("space", "tm")), P()),
        check_vma=False,
    )
```

time: 23.3 us -> 20.5 us (0.88)
  Pallas kernels: 20.1 us -> 17.3 us
    pallas_call x1, Pallas kernels: 20.1 us -> 17.3 us  [on_device(): pl.pallas_call(functools.partial(kernel, tm, space, low, high, nt, rows,...]
where the time goes in v2:
time: 20.5 us; the launch traced here: 20.3 us
  Pallas kernels  17.3 us (84%)
  local copies, waits for them, and re-layouts  2.39 us (12%)
  between operations  0.64 us (3%)
    pallas_call x1, Pallas kernels, on_device(): pl.pallas_call(functools.partial(kernel, tm, space, low, high, nt, rows,...  17.3 us
    unnamed x2, local copies, waits for them, and re-layouts  2.39 us

profile of v2, /device:TPU:0, one launch (start us, length us, event | category | flops | bytes accessed | tf_op | source)
XLA Modules:
  0.0 20.3 jit_solution(15633241315552079280)
XLA Ops:
  0.6 17.3 %shard_map.30 = (f32[2,256]{1,0:T(2,128)}, f32[1,3]{1,0:T(1,128)}) custom-call(f32[18,4,4,8,128]{4,3,2,1,0:T(8,128)} %bitcast.6), custom_call_target="tpu_custom_call" | custom-call | tf_op jit(solution)/shard_map/pallas_call | solution.py:279
  18.0 1.2 %copy.6 = f32[2,256]{1,0:T(2,128)} copy(f32[2,256]{1,0:T(2,128)} %get-tuple-element.8) | data formatting | bytes 4096
  19.2 1.1 %copy.7 = f32[3]{0:T(128)} copy(f32[3]{0:T(128)} %bitcast.7) | data formatting | bytes 24

commit v3 on v2

--- a/solution.py
+++ b/solution.py
@@ -259,6 +259,15 @@
         copy.wait_send()
 
 
+def hand_out(ploop, stats, ploop_out, stats_out, sem_a, sem_b):
+    first = pltpu.make_async_copy(ploop, ploop_out, sem_a)
+    second = pltpu.make_async_copy(stats, stats_out, sem_b)
+    first.start()
+    second.start()
+    first.wait()
+    second.wait()
+
+
 def on_device(tm, space, links):
     nt, sites = links.shape[3], links.shape[4]
     share = sites // tm
@@ -272,6 +281,7 @@
         view = jnp.pad(view, ((0, 0), (0, 0), (0, 0), (0, padded - share)))
     view = view.reshape(18, nt, tm * rows, LANES).transpose(0, 2, 1, 3)
     view = view.reshape(18, high, low, rows * nt, LANES)
+    view = pltpu.with_memory_space_constraint(view, pltpu.HBM)
     band, part = high * rows, high // 2 * rows
     count = tm * space
     f32 = jnp.float32
@@ -279,7 +289,7 @@
     ploop, stats = pl.pallas_call(
         functools.partial(kernel, tm, space, low, high, nt, rows, share, sites * space),
         out_shape=(jax.ShapeDtypeStruct((2, share), f32), jax.ShapeDtypeStruct((1, 3), f32)),
-        in_specs=[pl.BlockSpec(memory_space=pl.ANY)],
+        in_specs=[pl.BlockSpec(memory_space=pltpu.HBM)],
         out_specs=(pl.BlockSpec(memory_space=pltpu.VMEM), pl.BlockSpec(memory_space=pltpu.VMEM)),
         scratch_shapes=[
             pltpu.VMEM((low, 18, band * nt, LANES), f32),
@@ -302,8 +312,16 @@
             pltpu.SemaphoreType.DMA((high // 2,)),
             pltpu.SemaphoreType.DMA,
         ],
-        compiler_params=pltpu.CompilerParams(collective_id=0, has_side_effects=True),
+        compiler_params=pltpu.CompilerParams(collective_id=0, has_side_effects=True, vmem_limit_bytes=24 << 20),
     )(view)
+    ploop, stats = pl.pallas_call(
+        hand_out,
+        out_shape=(jax.ShapeDtypeStruct((2, share), f32), jax.ShapeDtypeStruct((1, 3), f32)),
+        in_specs=[pl.BlockSpec(memory_space=pltpu.VMEM)] * 2,
+        out_specs=[pl.BlockSpec(memory_space=pltpu.HBM)] * 2,
+        scratch_shapes=[pltpu.SemaphoreType.DMA, pltpu.SemaphoreType.DMA],
+        compiler_params=pltpu.CompilerParams(vmem_limit_bytes=1 << 20),
+    )(ploop, stats)
     return ploop, stats.reshape(3)
 
 

time: 20.5 us -> 18.1 us (0.88)
  local copies, waits for them, and re-layouts: 2.39 us -> 0 us
    unnamed x2 -> x0, local copies, waits for them, and re-layouts: 2.39 us -> none
    pallas_call x0 -> x1, Pallas kernels: none -> 0.6 us  [on_device(): pl.pallas_call(hand_out, out_shape=(jax.ShapeDtypeStruct((2, share), f32)...]
    pallas_call x1, Pallas kernels: 17.3 us -> 16.7 us  [on_device(): pl.pallas_call(functools.partial(kernel, tm, space, low, high, nt, rows,...]
where the time goes in v3:
time: 18.1 us; the launch traced here: 18 us
  Pallas kernels  17.3 us (96%)
  between operations  0.64 us (4%)
    pallas_call x1, Pallas kernels, on_device(): pl.pallas_call(functools.partial(kernel, tm, space, low, high, nt, rows,...  16.7 us
    pallas_call x1, Pallas kernels, on_device(): pl.pallas_call(hand_out, out_shape=(jax.ShapeDtypeStruct((2, share), f32)...  0.6 us

profile of v3, /device:TPU:0, one launch (start us, length us, event | category | flops | bytes accessed | tf_op | source)
XLA Modules:
  0.0 18.0 jit_solution(14339447674147173645)
XLA Ops:
  0.6 16.7 %shard_map.30 = (f32[2,256]{1,0:T(2,128)S(1)}, f32[1,3]{1,0:T(1,128)S(1)}) custom-call(f32[18,4,4,8,128]{4,3,2,1,0:T(8,128)} %bitcast.6), custom_call_target="tpu_custom_call" | custom-call | tf_op jit(solution)/shard_map/pallas_call | solution.py:289
  17.4 0.6 %shard_map.31 = (f32[2,256]{1,0:T(2,128)}, f32[1,3]{1,0:T(1,128)}) custom-call(f32[2,256]{1,0:T(2,128)S(1)} %get-tuple-element.6.ploop, f32[1,3]{1,0:T(1,128)S(1)} %get-tuple-element.7.stats), custom_call_target="tpu_custom_call" | custom-call | tf_op jit(solution)/shard_map/pallas_call | solution.py:317
